TPU v7x, 32 devices: a whole 2x2x4 slice. The times are simulated.
32 devices in a mesh: chan: 16 (over z, y, core), wall: 2 (over x).
Axes of the slice: x: 2, y: 2, z: 4, core: 2. Of those that a mesh axis runs over, the one named last changes fastest.
Arguments:
- coords: float32 [3, 16, 2, 4096], P(None, 'chan', 'wall'), as said below
- masses: float32 [16, 2, 4096], P('chan', 'wall'), may hold values from 0.5 to 2
- counts: int32 [16, 2, 16], P('chan', 'wall'), may hold values from 64 to 256
- lists: int32 [16, 2, 5, 16, 2], P('chan', 'wall'), may hold values from 0 to 47, as said below
Outputs:
- density: float32 [16, 2, 4096], P('chan', 'wall')
Inputs may be any that keep to these rules, and one draw needn't show every extreme that they name: `lists`: each row of 2 entries names different tiles; tile t of extended slab s is s * 16 + t, slab 0 the lower cross-wall neighbour, 1 the slab itself, 2 the upper neighbour. `coords`: channel components lie in [0, 1), cross-wall and depth components in [0, 8).
All inputs are finite; a program needn't handle non-finite values.
Results may differ from a plain program's by a relative error of at most 0.0003.
Values sent between devices are 32-bit elements; how exact they have to be, the bound alone decides.
A program may use at most 64 MiB of HBM per device.

v0:
```python
import math

import jax
import jax.numpy as jnp
from jax import lax
from jax.sharding import PartitionSpec as P

NB = 2
R = 4


def extended_2(block, sides, width):
    for axis, dim in sides:
        count = lax.axis_size(axis)
        forward = [(i, i + 1) for i in range(count - 1)]
        backward = [(target, source) for source, target in forward]
        low = lax.ppermute(
            lax.slice_in_dim(block, block.shape[dim] - width, None, axis=dim), axis, forward
        )
        high = lax.ppermute(lax.slice_in_dim(block, 0, width, axis=dim), axis, backward)
        block = jnp.concatenate([low, block, high], axis=dim)
    return block


def from_behind(block, axis, distance):
    devices = range(lax.axis_size(axis))
    route = [((i - distance) % len(devices), i) for i in devices]
    return lax.ppermute(block, axis, route)


def from_behind_2(block, axis, distance):
    devices = range(lax.axis_size(axis))
    route = [(i - distance, i) for i in devices if i - distance in devices]
    return lax.ppermute(block, axis, route)


def spline(scaled):
    return (jnp.maximum(2.0 - scaled, 0.0) ** 3 * 0.25 - jnp.maximum(1.0 - scaled, 0.0) ** 3) * (
        1.0 / math.pi
    )


def pair_block(own_block, partner, partner_rows, offset, with_back):
    tile_count = own_block.shape[1]
    tile_len = own_block.shape[2]
    list_len = partner_rows.shape[1]
    picked = jnp.take(partner, partner_rows.reshape(-1), axis=1).reshape(
        4, tile_count, list_len, tile_len
    )
    wall_lift = (partner_rows // tile_count - 1).astype(jnp.float32) * (2.0 * R)
    reach = float(R)

    def single_tile(inputs):
        own_tile, theirs, shift_y = inputs
        delta_x = own_tile[0][None, :, None] - (theirs[0][:, None, :] + offset)
        delta_y = own_tile[1][None, :, None] - (theirs[1][:, None, :] + shift_y[:, None, None])
        delta_z = own_tile[2][None, :, None] - theirs[2][:, None, :]
        distance = jnp.sqrt(delta_x * delta_x + delta_y * delta_y + delta_z * delta_z + 0.0001)
        weight = spline(distance / reach)
        gained = jnp.sum(weight * theirs[3][:, None, :], axis=(0, 2))
        handed = jnp.sum(weight * own_tile[3][None, :, None], axis=1)
        return (gained, handed)

    group = math.gcd(tile_count, 4)

    def grouped(values):
        return values.reshape((tile_count // group, group) + values.shape[1:])

    gained, handed = lax.map(
        jax.vmap(single_tile),
        (
            grouped(jnp.moveaxis(own_block, 1, 0)),
            grouped(jnp.moveaxis(picked, 1, 0)),
            grouped(wall_lift),
        ),
    )
    gained = gained.reshape(tile_count, tile_len)
    handed = handed.reshape(tile_count, list_len, tile_len)
    if not with_back:
        return (gained, None)
    onehot = (
        partner_rows.reshape(-1)[:, None] == jnp.arange(partner.shape[1], dtype=jnp.int32)[None, :]
    ).astype(jnp.float32)
    returned = jnp.dot(onehot.T, handed.reshape(-1, tile_len), precision=lax.Precision.HIGHEST)
    return (gained, returned)


def on_device(coords, masses, counts, lists):
    tile_count = counts.shape[2]
    tile_len = masses.shape[2] // tile_count
    slots = jnp.arange(tile_len, dtype=jnp.int32)
    filled = (slots[None, :] < counts[0, 0][:, None]).astype(jnp.float32)
    weighted = masses.reshape(tile_count, tile_len) * filled
    packed = jnp.concatenate([coords, weighted.reshape(1, 1, 1, -1)], axis=0)
    extended = extended_2(packed, (("wall", 2),), 1)
    extended = extended.reshape(4, 3 * tile_count, tile_len)
    own_block = packed.reshape(4, tile_count, tile_len)
    partner_rows = lists[0, 0]
    density, unused_back = pair_block(own_block, extended, partner_rows[0], 0.0, False)
    returns = jnp.zeros((3 * tile_count, tile_len), jnp.float32)
    for step in range(1, R + 1):
        partner = from_behind(extended, "chan", -step)
        gained, handed = pair_block(own_block, partner, partner_rows[step], float(step), True)
        density = density + gained
        returns = returns + from_behind(handed, "chan", step)
    from_below = from_behind_2(returns[2 * tile_count :], "wall", 1)
    from_above = from_behind_2(returns[:tile_count], "wall", -1)
    total = density + returns[tile_count : 2 * tile_count] + from_below + from_above
    return (total * filled / (NB * tile_len)).reshape(1, 1, -1)


def solution(mesh):
    placed = (
        P(None, "chan", "wall", None),
        P("chan", "wall", None),
        P("chan", "wall", None),
        P("chan", "wall", None, None, None),
    )
    return jax.shard_map(
        on_device, mesh=mesh, in_specs=placed, out_specs=P("chan", "wall", None), check_vma=False
    )
```

profile of v0, /device:TPU:0, one launch (start us, length us, event | category | flops | bytes accessed | tf_op | source)
XLA Modules:
  0.0 103.7 jit_solution(12260350591247521337)
XLA Ops:
  0.0 0.8 iota_compare_fusion.4
  0.8 0.7 bitcast_select_fusion
  1.6 0.9 pad_maximum_fusion.2
  2.4 4.9 %collective-permute-start = (f32[4,1,1,4096]{3,2,1,0:T(1,128)S(1)}, f32[4,1,1,4096]{3,2,1,0:T(1,128)S(1)}, u32[]{:S(2)}, u32[]{:S(2)}) collective-permute-start(f32[4,1,1,4096]{3,2,1,0:T(1,128)S(1)} %pad_maximum_fusion.2), channel_id=1, source_target_pairs={{0,1},{2,3},{4,5},{6,7},{8,9},{10,11},{12,13},{14,15},{16,17},{18,... | collective-permute-start | bytes 196616 | tf_op jit(solution)/shard_map/ppermute | solution.py:17
  7.3 1.3 %collective-permute-start.1 = (f32[4,1,1,4096]{3,2,1,0:T(1,128)S(1)}, f32[4,1,1,4096]{3,2,1,0:T(1,128)S(1)}, u32[]{:S(2)}, u32[]{:S(2)}) collective-permute-start(f32[4,1,1,4096]{3,2,1,0:T(1,128)S(1)} %pad_maximum_fusion.2), channel_id=1, source_target_pairs={{1,0},{3,2},{5,4},{7,6},{9,8},{11,10},{13,12},{15,14},{17,16},{19,... | collective-permute-start | bytes 196616 | tf_op jit(solution)/shard_map/ppermute | solution.py:20
  8.6 0.8 fusion.68
  10.9 0.1 reduce
  11.3 2.2 %collective-permute-done.1 = f32[4,1,1,4096]{3,2,1,0:T(1,128)S(1)} collective-permute-done((f32[4,1,1,4096]{3,2,1,0:T(1,128)S(1)}, f32[4,1,1,4096]{3,2,1,0:T(1,128)S(1)}, u32[]{:S(2)}, u32[]{:S(2)}) %collective-permute-start.1) | collective-permute-done | bytes 65568 | tf_op jit(solution)/shard_map/ppermute | solution.py:20
  13.5 0.2 pad_maximum_fusion
  13.7 0.1 reshape.315
  13.8 0.1 copy.104
  14.0 1.7 %collective-permute-start.4 = (f32[4,48,256]{2,0,1:T(4,128)S(1)}, f32[4,48,256]{2,0,1:T(4,128)S(1)}, u32[]{:S(2)}, u32[]{:S(2)}) collective-permute-start(f32[4,48,256]{2,0,1:T(4,128)S(1)} %copy.104), channel_id=1, source_target_pairs={{6,0},{8,2},{10,4},{12,6},{14,8},{16,10},{18,12},{20,14},{22,16},{... | collective-permute-start | bytes 589832 | tf_op jit(solution)/shard_map/ppermute | solution.py:28
  15.6 3.0 %collective-permute-start.3 = (f32[4,48,256]{2,0,1:T(4,128)S(1)}, f32[4,48,256]{2,0,1:T(4,128)S(1)}, u32[]{:S(2)}, u32[]{:S(2)}) collective-permute-start(f32[4,48,256]{2,0,1:T(4,128)S(1)} %copy.104), channel_id=1, source_target_pairs={{4,0},{6,2},{8,4},{10,6},{12,8},{14,10},{16,12},{18,14},{20,16},{2... | collective-permute-start | bytes 589832 | tf_op jit(solution)/shard_map/ppermute | solution.py:28
  18.6 1.3 %collective-permute-start.2 = (f32[4,48,256]{2,0,1:T(4,128)S(1)}, f32[4,48,256]{2,0,1:T(4,128)S(1)}, u32[]{:S(2)}, u32[]{:S(2)}) collective-permute-start(f32[4,48,256]{2,0,1:T(4,128)S(1)} %copy.104), channel_id=1, source_target_pairs={{2,0},{4,2},{6,4},{8,6},{10,8},{12,10},{14,12},{16,14},{18,16},{20... | collective-permute-start | bytes 589832 | tf_op jit(solution)/shard_map/ppermute | solution.py:28
  19.9 0.4 collective-permute-start.5
  20.4 0.6 gather_fusion
  21.0 0.1 broadcast_select_fusion.4
  21.1 0.6 gather_fusion.3
  21.8 0.1 broadcast_select_fusion.1
  21.9 12.6 %while.61 = (s32[]{:T(128)}, f32[4,4,256]{2,1,0:T(4,128)S(1)}, f32[4,4,2,256]{3,2,1,0:T(2,128)S(1)}, f32[4,4,4,256]{3,1,2,0:T(4,128)S(1)}, f32[4,4,4,2,256]{4,2,...) while((s32[]{:T(128)}, f32[4,4,256]{2,1,0:T(4,128)S(1)}, f32[4,4,2,256]{3,2,1,0:T(2,128)S(1)}, ...), condition=%wide.region_14.16_spmd, body=%wide.region_11.15_spmd.sunk | while | flops 12587010 | bytes 348417 | solution.py:69
  22.0 0.1 copy.165
  22.2 2.8 %multiply_reduce_fusion.14 = (f32[4,2,256]{2,1,0:T(2,128)S(1)}, f32[4,256]{1,0:T(4,128)S(1)}) fusion(f32[4,256]{1,0:T(4,128)S(1)} %get-tuple-element.665, f32[4,2,256]{2,1,0:T(2,128)S(1)} %get-tuple-element.666, f32[4,256]{1,0:T(4,128)S(1)} %get-tuple-element.667, f32[4,2,256]{2,1,0:T(2,128)S(1)} %fusion.90, f32[4,256]{1,0:T(4,128)S(1)} %get-tuple-element.668, ...), kind=kLoop, calls=%fused_computation.77.clone.1 | loop fusion | flops 12579840 | bytes 61440 | tf_op jit(solution)/shard_map/while/body/eval_jaxpr/vmap()/reduce_sum | solution.py:61
  25.1 0.1 copy.165
  25.3 2.8 %multiply_reduce_fusion.14 = (f32[4,2,256]{2,1,0:T(2,128)S(1)}, f32[4,256]{1,0:T(4,128)S(1)}) fusion(f32[4,256]{1,0:T(4,128)S(1)} %get-tuple-element.665, f32[4,2,256]{2,1,0:T(2,128)S(1)} %get-tuple-element.666, f32[4,256]{1,0:T(4,128)S(1)} %get-tuple-element.667, f32[4,2,256]{2,1,0:T(2,128)S(1)} %fusion.90, f32[4,256]{1,0:T(4,128)S(1)} %get-tuple-element.668, ...), kind=kLoop, calls=%fused_computation.77.clone.1 | loop fusion | flops 12579840 | bytes 61440 | tf_op jit(solution)/shard_map/while/body/eval_jaxpr/vmap()/reduce_sum | solution.py:61
  28.5 2.8 %multiply_reduce_fusion.14 = (f32[4,2,256]{2,1,0:T(2,128)S(1)}, f32[4,256]{1,0:T(4,128)S(1)}) fusion(f32[4,256]{1,0:T(4,128)S(1)} %get-tuple-element.665, f32[4,2,256]{2,1,0:T(2,128)S(1)} %get-tuple-element.666, f32[4,256]{1,0:T(4,128)S(1)} %get-tuple-element.667, f32[4,2,256]{2,1,0:T(2,128)S(1)} %fusion.90, f32[4,256]{1,0:T(4,128)S(1)} %get-tuple-element.668, ...), kind=kLoop, calls=%fused_computation.77.clone.1 | loop fusion | flops 12579840 | bytes 61440 | tf_op jit(solution)/shard_map/while/body/eval_jaxpr/vmap()/reduce_sum | solution.py:61
  31.6 2.8 %multiply_reduce_fusion.14 = (f32[4,2,256]{2,1,0:T(2,128)S(1)}, f32[4,256]{1,0:T(4,128)S(1)}) fusion(f32[4,256]{1,0:T(4,128)S(1)} %get-tuple-element.665, f32[4,2,256]{2,1,0:T(2,128)S(1)} %get-tuple-element.666, f32[4,256]{1,0:T(4,128)S(1)} %get-tuple-element.667, f32[4,2,256]{2,1,0:T(2,128)S(1)} %fusion.90, f32[4,256]{1,0:T(4,128)S(1)} %get-tuple-element.668, ...), kind=kLoop, calls=%fused_computation.77.clone.1 | loop fusion | flops 12579840 | bytes 61440 | tf_op jit(solution)/shard_map/while/body/eval_jaxpr/vmap()/reduce_sum | solution.py:61
  34.5 0.6 gather_fusion.2
  35.1 0.1 broadcast_select_fusion.2
  35.2 12.6 %while.60 = (s32[]{:T(128)}, f32[4,4,256]{2,1,0:T(4,128)S(1)}, f32[4,4,2,256]{3,2,1,0:T(2,128)S(1)}, f32[4,4,4,256]{3,1,2,0:T(4,128)S(1)}, f32[4,4,4,2,256]{4,2,...) while((s32[]{:T(128)}, f32[4,4,256]{2,1,0:T(4,128)S(1)}, f32[4,4,2,256]{3,2,1,0:T(2,128)S(1)}, ...), condition=%wide.region_10.12_spmd, body=%wide.region_7.11_spmd.sunk | while | flops 12587010 | bytes 348417 | solution.py:69
  35.5 2.8 %multiply_reduce_fusion.13 = (f32[4,2,256]{2,1,0:T(2,128)S(1)}, f32[4,256]{1,0:T(4,128)S(1)}) fusion(f32[4,256]{1,0:T(4,128)S(1)} %get-tuple-element.650, f32[4,2,256]{2,1,0:T(2,128)S(1)} %get-tuple-element.651, f32[4,256]{1,0:T(4,128)S(1)} %get-tuple-element.652, f32[4,2,256]{2,1,0:T(2,128)S(1)} %fusion.88, f32[4,256]{1,0:T(4,128)S(1)} %get-tuple-element.653, ...), kind=kLoop, calls=%fused_computation.53.clone.1 | loop fusion | flops 12579840 | bytes 61440 | tf_op jit(solution)/shard_map/while/body/eval_jaxpr/vmap()/reduce_sum | solution.py:61
  38.7 2.8 %multiply_reduce_fusion.13 = (f32[4,2,256]{2,1,0:T(2,128)S(1)}, f32[4,256]{1,0:T(4,128)S(1)}) fusion(f32[4,256]{1,0:T(4,128)S(1)} %get-tuple-element.650, f32[4,2,256]{2,1,0:T(2,128)S(1)} %get-tuple-element.651, f32[4,256]{1,0:T(4,128)S(1)} %get-tuple-element.652, f32[4,2,256]{2,1,0:T(2,128)S(1)} %fusion.88, f32[4,256]{1,0:T(4,128)S(1)} %get-tuple-element.653, ...), kind=kLoop, calls=%fused_computation.53.clone.1 | loop fusion | flops 12579840 | bytes 61440 | tf_op jit(solution)/shard_map/while/body/eval_jaxpr/vmap()/reduce_sum | solution.py:61
  41.8 2.8 %multiply_reduce_fusion.13 = (f32[4,2,256]{2,1,0:T(2,128)S(1)}, f32[4,256]{1,0:T(4,128)S(1)}) fusion(f32[4,256]{1,0:T(4,128)S(1)} %get-tuple-element.650, f32[4,2,256]{2,1,0:T(2,128)S(1)} %get-tuple-element.651, f32[4,256]{1,0:T(4,128)S(1)} %get-tuple-element.652, f32[4,2,256]{2,1,0:T(2,128)S(1)} %fusion.88, f32[4,256]{1,0:T(4,128)S(1)} %get-tuple-element.653, ...), kind=kLoop, calls=%fused_computation.53.clone.1 | loop fusion | flops 12579840 | bytes 61440 | tf_op jit(solution)/shard_map/while/body/eval_jaxpr/vmap()/reduce_sum | solution.py:61
  45.0 2.8 %multiply_reduce_fusion.13 = (f32[4,2,256]{2,1,0:T(2,128)S(1)}, f32[4,256]{1,0:T(4,128)S(1)}) fusion(f32[4,256]{1,0:T(4,128)S(1)} %get-tuple-element.650, f32[4,2,256]{2,1,0:T(2,128)S(1)} %get-tuple-element.651, f32[4,256]{1,0:T(4,128)S(1)} %get-tuple-element.652, f32[4,2,256]{2,1,0:T(2,128)S(1)} %fusion.88, f32[4,256]{1,0:T(4,128)S(1)} %get-tuple-element.653, ...), kind=kLoop, calls=%fused_computation.53.clone.1 | loop fusion | flops 12579840 | bytes 61440 | tf_op jit(solution)/shard_map/while/body/eval_jaxpr/vmap()/reduce_sum | solution.py:61
  47.8 0.6 gather_fusion.1
  48.5 0.1 broadcast_select_fusion.3
  48.6 12.6 %while.59 = (s32[]{:T(128)}, f32[4,4,256]{2,1,0:T(4,128)S(1)}, f32[4,4,2,256]{3,2,1,0:T(2,128)S(1)}, f32[4,4,4,256]{3,1,2,0:T(4,128)S(1)}, f32[4,4,4,2,256]{4,2,...) while((s32[]{:T(128)}, f32[4,4,256]{2,1,0:T(4,128)S(1)}, f32[4,4,2,256]{3,2,1,0:T(2,128)S(1)}, ...), condition=%wide.region_6.8_spmd, body=%wide.region_3.7_spmd.sunk | while | flops 12587010 | bytes 348417 | solution.py:69
  48.9 2.8 %multiply_reduce_fusion.12 = (f32[4,2,256]{2,1,0:T(2,128)S(1)}, f32[4,256]{1,0:T(4,128)S(1)}) fusion(f32[4,256]{1,0:T(4,128)S(1)} %get-tuple-element.635, f32[4,2,256]{2,1,0:T(2,128)S(1)} %get-tuple-element.636, f32[4,256]{1,0:T(4,128)S(1)} %get-tuple-element.637, f32[4,2,256]{2,1,0:T(2,128)S(1)} %fusion.86, f32[4,256]{1,0:T(4,128)S(1)} %get-tuple-element.638, ...), kind=kLoop, calls=%fused_computation.29.clone.1 | loop fusion | flops 12579840 | bytes 61440 | tf_op jit(solution)/shard_map/while/body/eval_jaxpr/vmap()/reduce_sum | solution.py:61
  52.0 2.8 %multiply_reduce_fusion.12 = (f32[4,2,256]{2,1,0:T(2,128)S(1)}, f32[4,256]{1,0:T(4,128)S(1)}) fusion(f32[4,256]{1,0:T(4,128)S(1)} %get-tuple-element.635, f32[4,2,256]{2,1,0:T(2,128)S(1)} %get-tuple-element.636, f32[4,256]{1,0:T(4,128)S(1)} %get-tuple-element.637, f32[4,2,256]{2,1,0:T(2,128)S(1)} %fusion.86, f32[4,256]{1,0:T(4,128)S(1)} %get-tuple-element.638, ...), kind=kLoop, calls=%fused_computation.29.clone.1 | loop fusion | flops 12579840 | bytes 61440 | tf_op jit(solution)/shard_map/while/body/eval_jaxpr/vmap()/reduce_sum | solution.py:61
  55.2 2.8 %multiply_reduce_fusion.12 = (f32[4,2,256]{2,1,0:T(2,128)S(1)}, f32[4,256]{1,0:T(4,128)S(1)}) fusion(f32[4,256]{1,0:T(4,128)S(1)} %get-tuple-element.635, f32[4,2,256]{2,1,0:T(2,128)S(1)} %get-tuple-element.636, f32[4,256]{1,0:T(4,128)S(1)} %get-tuple-element.637, f32[4,2,256]{2,1,0:T(2,128)S(1)} %fusion.86, f32[4,256]{1,0:T(4,128)S(1)} %get-tuple-element.638, ...), kind=kLoop, calls=%fused_computation.29.clone.1 | loop fusion | flops 12579840 | bytes 61440 | tf_op jit(solution)/shard_map/while/body/eval_jaxpr/vmap()/reduce_sum | solution.py:61
  58.3 2.8 %multiply_reduce_fusion.12 = (f32[4,2,256]{2,1,0:T(2,128)S(1)}, f32[4,256]{1,0:T(4,128)S(1)}) fusion(f32[4,256]{1,0:T(4,128)S(1)} %get-tuple-element.635, f32[4,2,256]{2,1,0:T(2,128)S(1)} %get-tuple-element.636, f32[4,256]{1,0:T(4,128)S(1)} %get-tuple-element.637, f32[4,2,256]{2,1,0:T(2,128)S(1)} %fusion.86, f32[4,256]{1,0:T(4,128)S(1)} %get-tuple-element.638, ...), kind=kLoop, calls=%fused_computation.29.clone.1 | loop fusion | flops 12579840 | bytes 61440 | tf_op jit(solution)/shard_map/while/body/eval_jaxpr/vmap()/reduce_sum | solution.py:61
  61.2 0.6 gather_fusion.4
  61.8 0.1 broadcast_select_fusion
  61.9 12.6 %while.62 = (s32[]{:T(128)}, f32[4,4,256]{2,1,0:T(4,128)S(1)}, f32[4,4,2,256]{3,2,1,0:T(2,128)S(1)}, f32[4,4,4,256]{3,1,2,0:T(4,128)S(1)}, f32[4,4,4,2,256]{4,2,...) while((s32[]{:T(128)}, f32[4,4,256]{2,1,0:T(4,128)S(1)}, f32[4,4,2,256]{3,2,1,0:T(2,128)S(1)}, ...), condition=%wide.region_18.20_spmd, body=%wide.region_15.19_spmd.sunk | while | flops 12587010 | bytes 348417 | solution.py:69
  62.2 2.8 %multiply_reduce_fusion.15 = (f32[4,2,256]{2,1,0:T(2,128)S(1)}, f32[4,256]{1,0:T(4,128)S(1)}) fusion(f32[4,256]{1,0:T(4,128)S(1)} %get-tuple-element.680, f32[4,2,256]{2,1,0:T(2,128)S(1)} %get-tuple-element.681, f32[4,256]{1,0:T(4,128)S(1)} %get-tuple-element.682, f32[4,2,256]{2,1,0:T(2,128)S(1)} %fusion.92, f32[4,256]{1,0:T(4,128)S(1)} %get-tuple-element.683, ...), kind=kLoop, calls=%fused_computation.101.clone.1 | loop fusion | flops 12579840 | bytes 61440 | tf_op jit(solution)/shard_map/while/body/eval_jaxpr/vmap()/reduce_sum | solution.py:61
  65.4 2.8 %multiply_reduce_fusion.15 = (f32[4,2,256]{2,1,0:T(2,128)S(1)}, f32[4,256]{1,0:T(4,128)S(1)}) fusion(f32[4,256]{1,0:T(4,128)S(1)} %get-tuple-element.680, f32[4,2,256]{2,1,0:T(2,128)S(1)} %get-tuple-element.681, f32[4,256]{1,0:T(4,128)S(1)} %get-tuple-element.682, f32[4,2,256]{2,1,0:T(2,128)S(1)} %fusion.92, f32[4,256]{1,0:T(4,128)S(1)} %get-tuple-element.683, ...), kind=kLoop, calls=%fused_computation.101.clone.1 | loop fusion | flops 12579840 | bytes 61440 | tf_op jit(solution)/shard_map/while/body/eval_jaxpr/vmap()/reduce_sum | solution.py:61
  68.5 2.8 %multiply_reduce_fusion.15 = (f32[4,2,256]{2,1,0:T(2,128)S(1)}, f32[4,256]{1,0:T(4,128)S(1)}) fusion(f32[4,256]{1,0:T(4,128)S(1)} %get-tuple-element.680, f32[4,2,256]{2,1,0:T(2,128)S(1)} %get-tuple-element.681, f32[4,256]{1,0:T(4,128)S(1)} %get-tuple-element.682, f32[4,2,256]{2,1,0:T(2,128)S(1)} %fusion.92, f32[4,256]{1,0:T(4,128)S(1)} %get-tuple-element.683, ...), kind=kLoop, calls=%fused_computation.101.clone.1 | loop fusion | flops 12579840 | bytes 61440 | tf_op jit(solution)/shard_map/while/body/eval_jaxpr/vmap()/reduce_sum | solution.py:61
  71.7 2.8 %multiply_reduce_fusion.15 = (f32[4,2,256]{2,1,0:T(2,128)S(1)}, f32[4,256]{1,0:T(4,128)S(1)}) fusion(f32[4,256]{1,0:T(4,128)S(1)} %get-tuple-element.680, f32[4,2,256]{2,1,0:T(2,128)S(1)} %get-tuple-element.681, f32[4,256]{1,0:T(4,128)S(1)} %get-tuple-element.682, f32[4,2,256]{2,1,0:T(2,128)S(1)} %fusion.92, f32[4,256]{1,0:T(4,128)S(1)} %get-tuple-element.683, ...), kind=kLoop, calls=%fused_computation.101.clone.1 | loop fusion | flops 12579840 | bytes 61440 | tf_op jit(solution)/shard_map/while/body/eval_jaxpr/vmap()/reduce_sum | solution.py:61
  74.5 0.3 fusion.34
  74.8 1.7 %collective-permute-start.6 = (f32[48,256]{1,0:T(8,128)S(1)}, f32[48,256]{1,0:T(8,128)S(1)}, u32[]{:S(2)}, u32[]{:S(2)}) collective-permute-start(f32[48,256]{1,0:T(8,128)S(1)} %fusion.34), channel_id=1, source_target_pairs={{30,0},{0,2},{2,4},{4,6},{6,8},{8,10},{10,12},{12,14},{14,16},{16,... | collective-permute-start | bytes 147464 | tf_op jit(solution)/shard_map/ppermute | solution.py:28
  76.5 0.3 fusion.35
  76.8 0.9 collective-permute-start.7
  77.8 0.3 fusion.36
  78.1 2.5 %collective-permute-start.8 = (f32[48,256]{1,0:T(8,128)S(1)}, f32[48,256]{1,0:T(8,128)S(1)}, u32[]{:S(2)}, u32[]{:S(2)}) collective-permute-start(f32[48,256]{1,0:T(8,128)S(1)} %fusion.36), channel_id=1, source_target_pairs={{26,0},{28,2},{30,4},{0,6},{2,8},{4,10},{6,12},{8,14},{10,16},{12,... | collective-permute-start | bytes 147464 | tf_op jit(solution)/shard_map/ppermute | solution.py:28
  80.6 0.3 fusion.37
  80.9 1.6 %collective-permute-start.9 = (f32[48,256]{1,0:T(8,128)S(1)}, f32[48,256]{1,0:T(8,128)S(1)}, u32[]{:S(2)}, u32[]{:S(2)}) collective-permute-start(f32[48,256]{1,0:T(8,128)S(1)} %fusion.37), channel_id=1, source_target_pairs={{24,0},{26,2},{28,4},{30,6},{0,8},{2,10},{4,12},{6,14},{8,16},{10,... | collective-permute-start | bytes 147464 | tf_op jit(solution)/shard_map/ppermute | solution.py:28
  82.5 12.4 %while.58 = (s32[]{:T(128)}, f32[4,4,256]{2,1,0:T(4,128)S(1)}, f32[4,4,4,256]{3,1,2,0:T(4,128)S(1)}, f32[4,4,4,2,256]{4,2,3,1,0:T(4,128)S(1)}, f32[4,4,2]{1,0,2:T(4,128)S(1)}, /*index=5*/s32[]{:T(128)}) while((s32[]{:T(128)}, f32[4,4,256]{2,1,0:T(4,128)S(1)}, f32[4,4,4,256]{3,1,2,0:T(4,128)S(1)}, f32[4,4,4,2,256]{4,2,3,1,0:T(4,128)S(1)}, ...), condition=%wide.region_2.4_spmd, body=%wide.region_0.3_spmd.sunk | while | flops 11537410 | bytes 311541 | solution.py:69
  82.8 2.8 %fusion.84 = f32[4,256]{1,0:T(4,128)S(1)} fusion(f32[4,2,256]{2,1,0:T(2,128)S(1)} %get-tuple-element.623, f32[4,2,256]{2,1,0:T(2,128)S(1)} %get-tuple-element.624, f32[4,256]{1,0:T(4,128)S(1)} %get-tuple-element.625, f32[4,2,256]{2,1,0:T(2,128)S(1)} %fusion.83, f32[4,256]{1,0:T(4,128)S(1)} %get-tuple-element.626, ...), kind=kLoop, calls=%fused_computation.10.clone.1 | loop fusion | flops 11533312 | bytes 49152 | tf_op jit(solution)/shard_map/while/body/eval_jaxpr/vmap()/reduce_sum | solution.py:60
  85.9 2.8 %fusion.84 = f32[4,256]{1,0:T(4,128)S(1)} fusion(f32[4,2,256]{2,1,0:T(2,128)S(1)} %get-tuple-element.623, f32[4,2,256]{2,1,0:T(2,128)S(1)} %get-tuple-element.624, f32[4,256]{1,0:T(4,128)S(1)} %get-tuple-element.625, f32[4,2,256]{2,1,0:T(2,128)S(1)} %fusion.83, f32[4,256]{1,0:T(4,128)S(1)} %get-tuple-element.626, ...), kind=kLoop, calls=%fused_computation.10.clone.1 | loop fusion | flops 11533312 | bytes 49152 | tf_op jit(solution)/shard_map/while/body/eval_jaxpr/vmap()/reduce_sum | solution.py:60
  89.0 2.8 %fusion.84 = f32[4,256]{1,0:T(4,128)S(1)} fusion(f32[4,2,256]{2,1,0:T(2,128)S(1)} %get-tuple-element.623, f32[4,2,256]{2,1,0:T(2,128)S(1)} %get-tuple-element.624, f32[4,256]{1,0:T(4,128)S(1)} %get-tuple-element.625, f32[4,2,256]{2,1,0:T(2,128)S(1)} %fusion.83, f32[4,256]{1,0:T(4,128)S(1)} %get-tuple-element.626, ...), kind=kLoop, calls=%fused_computation.10.clone.1 | loop fusion | flops 11533312 | bytes 49152 | tf_op jit(solution)/shard_map/while/body/eval_jaxpr/vmap()/reduce_sum | solution.py:60
  92.1 2.8 %fusion.84 = f32[4,256]{1,0:T(4,128)S(1)} fusion(f32[4,2,256]{2,1,0:T(2,128)S(1)} %get-tuple-element.623, f32[4,2,256]{2,1,0:T(2,128)S(1)} %get-tuple-element.624, f32[4,256]{1,0:T(4,128)S(1)} %get-tuple-element.625, f32[4,2,256]{2,1,0:T(2,128)S(1)} %fusion.83, f32[4,256]{1,0:T(4,128)S(1)} %get-tuple-element.626, ...), kind=kLoop, calls=%fused_computation.10.clone.1 | loop fusion | flops 11533312 | bytes 49152 | tf_op jit(solution)/shard_map/while/body/eval_jaxpr/vmap()/reduce_sum | solution.py:60
  95.0 2.3 %collective-permute-start.10 = (f32[16,256]{1,0:T(8,128)S(1)}, f32[16,256]{1,0:T(8,128)S(1)}, u32[]{:S(2)}, u32[]{:S(2)}) collective-permute-start(f32[16,256]{1,0:T(8,128)S(1)} %get-tuple-element.419), channel_id=1, source_target_pairs={{0,1},{2,3},{4,5},{6,7},{8,9},{10,11},{12,13},{14,15},{16,17},{18,... | collective-permute-start | bytes 49160 | tf_op jit(solution)/shard_map/ppermute | solution.py:34
  97.4 1.3 %collective-permute-start.11 = (f32[16,256]{1,0:T(8,128)S(1)}, f32[16,256]{1,0:T(8,128)S(1)}, u32[]{:S(2)}, u32[]{:S(2)}) collective-permute-start(f32[16,256]{1,0:T(8,128)S(1)} %get-tuple-element.420), channel_id=1, source_target_pairs={{1,0},{3,2},{5,4},{7,6},{9,8},{11,10},{13,12},{15,14},{17,16},{19,... | collective-permute-start | bytes 49160 | tf_op jit(solution)/shard_map/ppermute | solution.py:34
  98.8 4.2 %collective-permute-done.11 = f32[16,256]{1,0:T(8,128)S(1)} collective-permute-done((f32[16,256]{1,0:T(8,128)S(1)}, f32[16,256]{1,0:T(8,128)S(1)}, u32[]{:S(2)}, u32[]{:S(2)}) %collective-permute-start.11) | collective-permute-done | bytes 16416 | tf_op jit(solution)/shard_map/ppermute | solution.py:34
  103.1 0.6 reshape.326
  (267 shorter events, 6.9 us)
Async XLA Ops:
  0.0 10.8 %copy-start.2 = (s32[1,1,16]{2,1,0:T(1,128)S(1)}, s32[1,1,16]{2,1,0:T(1,128)}, u32[]{:S(2)}) copy-start(s32[1,1,16]{2,1,0:T(1,128)} %param.18) | copy-start | bytes 196
  0.0 10.8 %copy-start.1 = (f32[1,1,4096]{2,1,0:T(1,128)S(1)}, f32[1,1,4096]{2,1,0:T(1,128)}, u32[]{:S(2)}) copy-start(f32[1,1,4096]{2,1,0:T(1,128)} %param.17) | copy-start | bytes 49156
  0.0 10.9 %copy-start = (f32[3,1,1,4096]{3,2,1,0:T(1,128)S(1)}, f32[3,1,1,4096]{3,2,1,0:T(1,128)}, u32[]{:S(2)}) copy-start(f32[3,1,1,4096]{3,2,1,0:T(1,128)} %param.16) | copy-start | bytes 147460
  2.4 8.8 %collective-permute-start = (f32[4,1,1,4096]{3,2,1,0:T(1,128)S(1)}, f32[4,1,1,4096]{3,2,1,0:T(1,128)S(1)}, u32[]{:S(2)}, u32[]{:S(2)}) collective-permute-start(f32[4,1,1,4096]{3,2,1,0:T(1,128)S(1)} %pad_maximum_fusion.2), channel_id=1, source_target_pairs={{0,1},{2,3},{4,5},{6,7},{8,9},{10,11},{12,13},{14,15},{16,17},{18,... | collective-permute-start | bytes 196616 | tf_op jit(solution)/shard_map/ppermute | solution.py:17
  7.3 6.2 %collective-permute-start.1 = (f32[4,1,1,4096]{3,2,1,0:T(1,128)S(1)}, f32[4,1,1,4096]{3,2,1,0:T(1,128)S(1)}, u32[]{:S(2)}, u32[]{:S(2)}) collective-permute-start(f32[4,1,1,4096]{3,2,1,0:T(1,128)S(1)} %pad_maximum_fusion.2), channel_id=1, source_target_pairs={{1,0},{3,2},{5,4},{7,6},{9,8},{11,10},{13,12},{15,14},{17,16},{19,... | collective-permute-start | bytes 196616 | tf_op jit(solution)/shard_map/ppermute | solution.py:20
  14.0 7.2 %collective-permute-start.4 = (f32[4,48,256]{2,0,1:T(4,128)S(1)}, f32[4,48,256]{2,0,1:T(4,128)S(1)}, u32[]{:S(2)}, u32[]{:S(2)}) collective-permute-start(f32[4,48,256]{2,0,1:T(4,128)S(1)} %copy.104), channel_id=1, source_target_pairs={{6,0},{8,2},{10,4},{12,6},{14,8},{16,10},{18,12},{20,14},{22,16},{... | collective-permute-start | bytes 589832 | tf_op jit(solution)/shard_map/ppermute | solution.py:28
  15.6 18.8 %collective-permute-start.3 = (f32[4,48,256]{2,0,1:T(4,128)S(1)}, f32[4,48,256]{2,0,1:T(4,128)S(1)}, u32[]{:S(2)}, u32[]{:S(2)}) collective-permute-start(f32[4,48,256]{2,0,1:T(4,128)S(1)} %copy.104), channel_id=1, source_target_pairs={{4,0},{6,2},{8,4},{10,6},{12,8},{14,10},{16,12},{18,14},{20,16},{2... | collective-permute-start | bytes 589832 | tf_op jit(solution)/shard_map/ppermute | solution.py:28
  18.6 29.2 %collective-permute-start.2 = (f32[4,48,256]{2,0,1:T(4,128)S(1)}, f32[4,48,256]{2,0,1:T(4,128)S(1)}, u32[]{:S(2)}, u32[]{:S(2)}) collective-permute-start(f32[4,48,256]{2,0,1:T(4,128)S(1)} %copy.104), channel_id=1, source_target_pairs={{2,0},{4,2},{6,4},{8,6},{10,8},{12,10},{14,12},{16,14},{18,16},{20... | collective-permute-start | bytes 589832 | tf_op jit(solution)/shard_map/ppermute | solution.py:28
  19.9 41.2 %collective-permute-start.5 = (f32[4,48,256]{2,0,1:T(4,128)S(1)}, f32[4,48,256]{2,0,1:T(4,128)S(1)}, u32[]{:S(2)}, u32[]{:S(2)}) collective-permute-start(f32[4,48,256]{2,0,1:T(4,128)S(1)} %copy.104), channel_id=1, source_target_pairs={{8,0},{10,2},{12,4},{14,6},{16,8},{18,10},{20,12},{22,14},{24,16},... | collective-permute-start | bytes 589832 | tf_op jit(solution)/shard_map/ppermute | solution.py:28
  74.8 20.1 %collective-permute-start.6 = (f32[48,256]{1,0:T(8,128)S(1)}, f32[48,256]{1,0:T(8,128)S(1)}, u32[]{:S(2)}, u32[]{:S(2)}) collective-permute-start(f32[48,256]{1,0:T(8,128)S(1)} %fusion.34), channel_id=1, source_target_pairs={{30,0},{0,2},{2,4},{4,6},{6,8},{8,10},{10,12},{12,14},{14,16},{16,... | collective-permute-start | bytes 147464 | tf_op jit(solution)/shard_map/ppermute | solution.py:28
  76.8 18.1 %collective-permute-start.7 = (f32[48,256]{1,0:T(8,128)S(1)}, f32[48,256]{1,0:T(8,128)S(1)}, u32[]{:S(2)}, u32[]{:S(2)}) collective-permute-start(f32[48,256]{1,0:T(8,128)S(1)} %fusion.35), channel_id=1, source_target_pairs={{28,0},{30,2},{0,4},{2,6},{4,8},{6,10},{8,12},{10,14},{12,16},{14,... | collective-permute-start | bytes 147464 | tf_op jit(solution)/shard_map/ppermute | solution.py:28
  78.1 16.9 %collective-permute-start.8 = (f32[48,256]{1,0:T(8,128)S(1)}, f32[48,256]{1,0:T(8,128)S(1)}, u32[]{:S(2)}, u32[]{:S(2)}) collective-permute-start(f32[48,256]{1,0:T(8,128)S(1)} %fusion.36), channel_id=1, source_target_pairs={{26,0},{28,2},{30,4},{0,6},{2,8},{4,10},{6,12},{8,14},{10,16},{12,... | collective-permute-start | bytes 147464 | tf_op jit(solution)/shard_map/ppermute | solution.py:28
  80.9 14.1 %collective-permute-start.9 = (f32[48,256]{1,0:T(8,128)S(1)}, f32[48,256]{1,0:T(8,128)S(1)}, u32[]{:S(2)}, u32[]{:S(2)}) collective-permute-start(f32[48,256]{1,0:T(8,128)S(1)} %fusion.37), channel_id=1, source_target_pairs={{24,0},{26,2},{28,4},{30,6},{0,8},{2,10},{4,12},{6,14},{8,16},{10,... | collective-permute-start | bytes 147464 | tf_op jit(solution)/shard_map/ppermute | solution.py:28
  95.0 3.8 %collective-permute-start.10 = (f32[16,256]{1,0:T(8,128)S(1)}, f32[16,256]{1,0:T(8,128)S(1)}, u32[]{:S(2)}, u32[]{:S(2)}) collective-permute-start(f32[16,256]{1,0:T(8,128)S(1)} %get-tuple-element.419), channel_id=1, source_target_pairs={{0,1},{2,3},{4,5},{6,7},{8,9},{10,11},{12,13},{14,15},{16,17},{18,... | collective-permute-start | bytes 49160 | tf_op jit(solution)/shard_map/ppermute | solution.py:34
  97.4 5.6 %collective-permute-start.11 = (f32[16,256]{1,0:T(8,128)S(1)}, f32[16,256]{1,0:T(8,128)S(1)}, u32[]{:S(2)}, u32[]{:S(2)}) collective-permute-start(f32[16,256]{1,0:T(8,128)S(1)} %get-tuple-element.420), channel_id=1, source_target_pairs={{1,0},{3,2},{5,4},{7,6},{9,8},{11,10},{13,12},{15,14},{17,16},{19,... | collective-permute-start | bytes 49160 | tf_op jit(solution)/shard_map/ppermute | solution.py:34
where the time goes:
time: 104 us
  other arithmetic  61.6 us (59%)
  starting transfers between devices  23 us (22%)
  local copies, waits for them, and re-layouts  9.6 us (9%)
  waiting for transfers between devices  6.55 us (6%)
  loops' own time  1.3 us (1%)
  matrix products  1.15 us (1%)
    reduce_sum x16, other arithmetic, single_tile(): handed = jnp.sum(weight * own_tile[3][None, :, None], axis=1)  45 us
    ppermute x8, starting transfers between devices, from_behind(): return lax.ppermute(block, axis, route)  13.2 us
    reduce_sum x4, other arithmetic, single_tile(): gained = jnp.sum(weight * theirs[3][:, None, :], axis=(0, 2))  11.2 us
    ppermute x1, starting transfers between devices, extended_2(): lax.ppermute(lax.slice_in_dim(block, block.shape[dim] - width, None, axis...  4.87 us
    ppermute x2, waiting for transfers between devices, from_behind_2(): return lax.ppermute(block, axis, route)  4.3 us
    ppermute x2, starting transfers between devices, from_behind_2(): return lax.ppermute(block, axis, route)  3.63 us
    gather x5, local copies, waits for them, and re-layouts, pair_block(): jnp.take(partner, partner_rows.reshape(-1), axis=1)  3.15 us
    ppermute x1, waiting for transfers between devices, extended_2(): lax.ppermute(lax.slice_in_dim(block, 0, width, axis=dim), axis, backward)  2.22 us
  transfers between devices with their start and end apart: 12, of which 3 were waited for; matrix products, arithmetic and copies ran while one was open for 53% of the time, Pallas kernels for 0%

commit v1 on v0

v1 whole, which is shorter than its diff:
```python
import functools
import math

import jax
import jax.numpy as jnp
from jax import lax
from jax.experimental import pallas as pl
from jax.experimental.pallas import tpu as pltpu
from jax.sharding import PartitionSpec as P

NB = 2
R = 4
LANES = 128
ROWS = 64
MESH = pl.DeviceIdType.MESH


def wall_cases(wall, walls, flip):
    cases = []
    for s in range(3):
        other = wall + (1 - s if flip else s - 1)
        cases.append((s, other, jnp.logical_and(other >= 0, other < walls)))
    return cases


def gather_kernel(chans, walls, own_ref, ext_ref, send_sem, recv_sem, local_sem):
    chan = lax.axis_index("chan")
    wall = lax.axis_index("wall")
    valid = 1 + (wall > 0).astype(jnp.int32) + (wall < walls - 1).astype(jnp.int32)
    keep = pltpu.make_async_copy(own_ref, ext_ref.at[1], local_sem)
    keep.start()
    barrier = pltpu.get_barrier_semaphore()
    for s, other, there in wall_cases(wall, walls, False):
        @pl.when(there)
        def _(s=s, other=other):
            for k in range(R + 1):
                if k == 0 and s == 1:
                    continue
                pl.semaphore_signal(
                    barrier, inc=1, device_id=(lax.rem(chan + k, chans), other), device_id_type=MESH
                )
    pl.semaphore_wait(barrier, (R + 1) * valid - 1)

    def copy(k, s, other):
        return pltpu.make_async_remote_copy(
            src_ref=own_ref,
            dst_ref=ext_ref.at[k * 3 + s],
            send_sem=send_sem.at[k * 3 + s],
            recv_sem=recv_sem.at[k * 3 + s],
            device_id=(lax.rem(chan + chans - k, chans), other),
            device_id_type=MESH,
        )

    for k in range(R, -1, -1):
        for s, other, there in wall_cases(wall, walls, True):
            if k == 0 and s == 1:
                continue

            @pl.when(there)
            def _(k=k, s=s, other=other):
                copy(k, s, other).start()

    for k in range(R + 1):
        for s, other, there in wall_cases(wall, walls, False):
            if k == 0 and s == 1:
                continue

            @pl.when(there)
            def _(k=k, s=s, other=other):
                copy(k, s, other).wait_recv()

    for k in range(R + 1):
        for s, other, there in wall_cases(wall, walls, True):
            if k == 0 and s == 1:
                continue

            @pl.when(there)
            def _(k=k, s=s, other=other):
                copy(k, s, other).wait_send()
    keep.wait()


def gather(own, chans, walls):
    slots = (R + 1) * 3
    return pl.pallas_call(
        functools.partial(gather_kernel, chans, walls),
        out_shape=jax.ShapeDtypeStruct((slots,) + own.shape, own.dtype),
        in_specs=[pl.BlockSpec(memory_space=pltpu.VMEM)],
        out_specs=pl.BlockSpec(memory_space=pl.ANY),
        scratch_shapes=[
            pltpu.SemaphoreType.DMA((slots,)),
            pltpu.SemaphoreType.DMA((slots,)),
            pltpu.SemaphoreType.DMA,
        ],
        compiler_params=pltpu.CompilerParams(collective_id=0, has_side_effects=True),
    )(own)


def pair_kernel(
    walls,
    lists_ref,
    counts_ref,
    own_ref,
    ext_ref,
    gained_ref,
    handed_ref,
    cols,
    gacc,
    gains,
    hands,
    used,
    blocks_ref,
    sem,
):
    tiles, _, tile_len = own_ref.shape
    lane_blocks = tile_len // LANES
    list_len = lists_ref.shape[0] // ((R + 1) * tiles)
    wall = lax.axis_index("wall")
    filled = jnp.zeros((ext_ref.shape[0], LANES), jnp.float32)
    for h in range(lane_blocks):
        filled += (ext_ref[:, 3, h * LANES : (h + 1) * LANES] > 0.0).astype(jnp.float32)
    used[...] = jnp.transpose(filled, (1, 0))[:8].astype(jnp.int32)
    fetch = pltpu.make_async_copy(used, blocks_ref, sem)
    fetch.start()
    hands[...] = jnp.zeros_like(hands)
    fetch.wait()

    def own_tile(t, carry):
        turned = jnp.transpose(own_ref[t], (1, 0))
        for i in range(4):
            scale = 1.0 / R if i < 3 else 1.0
            cols[i] = jnp.broadcast_to(turned[:, i : i + 1] * scale, (tile_len, LANES))
        gacc[...] = jnp.zeros_like(gacc)
        groups = (counts_ref[t] + (ROWS - 1)) // ROWS

        def partner(m, carry):
            k = m // list_len
            j = m - k * list_len
            tile = lists_ref[(k * tiles + t) * list_len + j]
            at = k * 3 * tiles + tile
            slab = tile // tiles
            edge = wall + slab - 1
            real = jnp.logical_and(edge >= 0, edge < walls)
            blocks = jnp.where(real, blocks_ref[0, at], 0)
            lift = (slab - 1).astype(jnp.float32) * 2.0
            ahead = k.astype(jnp.float32) * (1.0 / R)

            def run(width):
                row = ext_ref[at]
                lanes = [pl.ds(h * LANES, LANES) for h in range(width)]

                def spread(i, h, scale, shift):
                    value = row[i : i + 1, h * LANES : (h + 1) * LANES]
                    if scale is not None:
                        value = value * scale + shift
                    return jnp.broadcast_to(value, (8, LANES))

                theirs = [
                    (
                        spread(0, h, 1.0 / R, ahead),
                        spread(1, h, 1.0 / R, lift),
                        spread(2, h, 1.0 / R, 0.0),
                        spread(3, h, None, None),
                    )
                    for h in range(width)
                ]

                def rows(g, sums):
                    sums = list(sums)
                    base = g * ROWS
                    for r in range(0, ROWS, 8):
                        here = pl.ds(pl.multiple_of(base + r, 8), 8)
                        ax, ay, az, aw = (cols[i, here, :] for i in range(4))
                        total = None
                        for h in range(width):
                            bx, by, bz, bw = theirs[h]
                            dx, dy, dz = ax - bx, ay - by, az - bz
                            square = dx * dx + dy * dy + (dz * dz + 0.0001 / (R * R))
                            q = square * lax.rsqrt(square)
                            outer = jnp.maximum(2.0 - q, 0.0)
                            inner = jnp.maximum(1.0 - q, 0.0)
                            weight = outer * outer * outer - (inner * inner) * (inner * 4.0)
                            part = weight * bw
                            total = part if total is None else total + part
                            sums[h] = sums[h] + weight * aw
                        gacc[here, :] += total
                    return tuple(sums)

                zero = jnp.zeros((8, LANES), jnp.float32)
                sums = lax.fori_loop(0, groups, rows, (zero,) * width)
                for h in range(width):
                    hands[at, :, lanes[h]] += sums[h]

            for width in range(1, lane_blocks + 1):
                pl.when(blocks == width)(functools.partial(run, width))
            return carry

        lax.fori_loop(0, (R + 1) * list_len, partner, 0)
        gains[t] = jnp.sum(
            jnp.transpose(gacc[...], (1, 0)).reshape(LANES // 8, 8, tile_len), axis=0
        )
        return carry

    lax.fori_loop(0, tiles, own_tile, 0)
    gained_ref[...] = jnp.sum(gains[...], axis=1)
    handed_ref[...] = jnp.sum(hands[...], axis=1)


def pairs(lists, counts, own, ext, walls):
    tiles, _, tile_len = own.shape
    smem = pl.BlockSpec(memory_space=pltpu.SMEM)
    vmem = pl.BlockSpec(memory_space=pltpu.VMEM)
    return pl.pallas_call(
        functools.partial(pair_kernel, walls),
        out_shape=(
            jax.ShapeDtypeStruct((tiles, tile_len), jnp.float32),
            jax.ShapeDtypeStruct((ext.shape[0], tile_len), jnp.float32),
        ),
        in_specs=[smem, smem, vmem, vmem],
        out_specs=(vmem, vmem),
        scratch_shapes=[
            pltpu.VMEM((4, tile_len, LANES), jnp.float32),
            pltpu.VMEM((tile_len, LANES), jnp.float32),
            pltpu.VMEM((tiles, 8, tile_len), jnp.float32),
            pltpu.VMEM((ext.shape[0], 8, tile_len), jnp.float32),
            pltpu.VMEM((8, ext.shape[0]), jnp.int32),
            pltpu.SMEM((8, ext.shape[0]), jnp.int32),
            pltpu.SemaphoreType.DMA,
        ],
    )(lists, counts, own, ext)


def return_kernel(chans, walls, tiles, gained_ref, handed_ref, out_ref, held, send_sem, recv_sem):
    chan = lax.axis_index("chan")
    wall = lax.axis_index("wall")
    valid = 1 + (wall > 0).astype(jnp.int32) + (wall < walls - 1).astype(jnp.int32)
    barrier = pltpu.get_barrier_semaphore()
    for s, other, there in wall_cases(wall, walls, True):
        @pl.when(there)
        def _(s=s, other=other):
            for k in range(1, R + 1):
                pl.semaphore_signal(
                    barrier,
                    inc=1,
                    device_id=(lax.rem(chan + chans - k, chans), other),
                    device_id_type=MESH,
                )
    pl.semaphore_wait(barrier, R * valid)

    def copy(k, s, other):
        slot = (k - 1) * 3 + s
        return pltpu.make_async_remote_copy(
            src_ref=handed_ref.at[pl.ds((k * 3 + s) * tiles, tiles)],
            dst_ref=held.at[slot],
            send_sem=send_sem.at[slot],
            recv_sem=recv_sem.at[slot],
            device_id=(lax.rem(chan + k, chans), other),
            device_id_type=MESH,
        )

    for k in range(R, 0, -1):
        for s, other, there in wall_cases(wall, walls, False):
            @pl.when(there)
            def _(k=k, s=s, other=other):
                copy(k, s, other).start()

    out_ref[...] = gained_ref[...]
    for k in range(1, R + 1):
        for s, other, there in wall_cases(wall, walls, True):
            @pl.when(there)
            def _(k=k, s=s, other=other):
                copy(k, s, other).wait_recv()
                out_ref[...] += held[(k - 1) * 3 + s]

    for k in range(1, R + 1):
        for s, other, there in wall_cases(wall, walls, False):
            @pl.when(there)
            def _(k=k, s=s, other=other):
                copy(k, s, other).wait_send()


def hand_back(gained, handed, chans, walls):
    tiles, tile_len = gained.shape
    vmem = pl.BlockSpec(memory_space=pltpu.VMEM)
    return pl.pallas_call(
        functools.partial(return_kernel, chans, walls, tiles),
        out_shape=jax.ShapeDtypeStruct(gained.shape, gained.dtype),
        in_specs=[vmem, vmem],
        out_specs=vmem,
        scratch_shapes=[
            pltpu.VMEM((R * 3, tiles, tile_len), jnp.float32),
            pltpu.SemaphoreType.DMA((R * 3,)),
            pltpu.SemaphoreType.DMA((R * 3,)),
        ],
        compiler_params=pltpu.CompilerParams(collective_id=1, has_side_effects=True),
    )(gained, handed)


def on_device(chans, walls, coords, masses, counts, lists):
    tiles = counts.shape[2]
    tile_len = masses.shape[2] // tiles
    slots = jnp.arange(tile_len, dtype=jnp.int32)
    filled = (slots[None, :] < counts[0, 0][:, None]).astype(jnp.float32)
    weighted = masses.reshape(tiles, tile_len) * filled
    own = jnp.concatenate([coords.reshape(3, tiles, tile_len), weighted[None]], axis=0)
    own = jnp.moveaxis(own, 0, 1)
    ext = gather(own, chans, walls)
    gained, handed = pairs(
        lists.reshape(-1), counts.reshape(-1), own, ext.reshape(-1, 4, tile_len), walls
    )
    total = hand_back(gained, handed, chans, walls)
    scale = 1.0 / (4.0 * math.pi * NB * tile_len)
    return (total * filled * scale).reshape(1, 1, -1)


def solution(mesh):
    placed = (
        P(None, "chan", "wall", None),
        P("chan", "wall", None),
        P("chan", "wall", None),
        P("chan", "wall", None, None, None),
    )
    body = functools.partial(on_device, mesh.shape["chan"], mesh.shape["wall"])
    return jax.shard_map(
        body, mesh=mesh, in_specs=placed, out_specs=P("chan", "wall", None), check_vma=False
    )
```

time: 104 us -> 70.6 us (0.68)
  Pallas kernels: 0 us -> 66.8 us
  other arithmetic: 61.6 us -> 2.39 us
  starting transfers between devices: 23 us -> 0 us
  local copies, waits for them, and re-layouts: 9.6 us -> 2.12 us
  waiting for transfers between devices: 6.55 us -> 0 us
  loops' own time: 1.3 us -> 0 us
  matrix products: 1.15 us -> 0 us
    pallas_call x0 -> x3, Pallas kernels: none -> 66.8 us  [the longest x1 37.6 us: pairs(): pl.pallas_call(functools.partial(pair_kernel, walls), out_shape=(jax.Shap...]
    reduce_sum x20 -> x0, other arithmetic: 56.2 us -> none  [the longest x16 45 us: single_tile(): handed = jnp.sum(weight * own_tile[3][None, :, None], axis=1)]
    ppermute x12 -> x0, starting transfers between devices: 23 us -> none  [the longest x8 13.2 us: from_behind(): return lax.ppermute(block, axis, route)]
    ppermute x12 -> x0, waiting for transfers between devices: 6.55 us -> none  [the longest x2 4.3 us: from_behind_2(): return lax.ppermute(block, axis, route)]
    gather x5 -> x0, local copies, waits for them, and re-layouts: 3.15 us -> none  [pair_block(): jnp.take(partner, partner_rows.reshape(-1), axis=1)]
    add x21 -> x0, local copies, waits for them, and re-layouts: 1.87 us -> none  [the longest x20 1.86 us: single_tile(): theirs[1][:, None, :] + shift_y[:, None, None]]
    add x22 -> x0, other arithmetic: 1.55 us -> none  [the longest x20 1.53 us: single_tile(): theirs[1][:, None, :] + shift_y[:, None, None]]
    another operation x5 -> x0, loops' own time: 1.3 us -> none  [pair_block(): lax.map(jax.vmap(single_tile), (grouped(jnp.moveaxis(own_block, 1, 0)), g...]
  transfers between devices with their start and end apart: 12 -> 0, of which waited for: 3 -> 0; matrix products, arithmetic and copies ran while one was open for 53% -> 0% of each run, Pallas kernels for 0% -> 0%
where the time goes in v1:
time: 70.6 us; the launch traced here: 71.3 us
  Pallas kernels  66.8 us (95%)
  other arithmetic  2.39 us (3%)
  local copies, waits for them, and re-layouts  2.12 us (3%)
    pallas_call x1, Pallas kernels, pairs(): pl.pallas_call(functools.partial(pair_kernel, walls), out_shape=(jax.Shap...  37.6 us
    pallas_call x1, Pallas kernels, gather(): pl.pallas_call(functools.partial(gather_kernel, chans, walls), out_shape=...  18.4 us
    pallas_call x1, Pallas kernels, hand_back(): pl.pallas_call(functools.partial(return_kernel, chans, walls, tiles), out...  10.7 us

profile of v1, /device:TPU:0, one launch (start us, length us, event | category | flops | bytes accessed | tf_op | source)
XLA Modules:
  0.0 71.3 jit_solution(8059788153973683535)
XLA Ops:
  0.0 0.0 copy-start.2
  0.0 0.7 copy-done.2
  0.7 0.0 copy-start.1
  0.7 0.8 %compare_select_fusion = f32[1,16,256]{2,0,1:T(1,128)S(1)} fusion(f32[1,16,256]{2,0,1:T(1,128)} %bitcast.10, s32[16]{0:T(128)S(1)} %bitcast.12), kind=kLoop, calls=%fused_computation.1 | loop fusion | flops 8192 | bytes 32832 | tf_op jit(solution)/shard_map/mul | solution.py:304
  1.5 0.0 copy-done.1
  1.5 0.0 copy-start
  1.5 0.1 copy.5
  1.6 0.7 %reshape.65.lists_ref = s32[160]{0:T(256)} reshape(s32[1,1,5,16,2]{4,3,2,1,0:T(8,128)S(1)} %copy.5) | data formatting | bytes 1280 | tf_op jit(solution)/shard_map/reshape | solution.py:309
  2.3 0.0 copy-done
  2.3 0.1 reduce
  2.5 0.7 maximum_bitcast_fusion.own_ref
  3.1 18.4 %shard_map.46 = f32[15,16,4,256]{3,2,1,0:T(4,128)} custom-call(f32[16,4,256]{2,1,0:T(4,128)} %maximum_bitcast_fusion.own_ref), custom_call_target="tpu_custom_call" | custom-call | tf_op jit(solution)/shard_map/pallas_call | solution.py:85
  21.6 37.6 %shard_map.47 = (f32[16,256]{1,0:T(8,128)}, f32[240,256]{1,0:T(8,128)}) custom-call(s32[160]{0:T(256)} %reshape.65.lists_ref, s32[16]{0:T(128)} %bitcast.11, f32[16,4,256]{2,1,0:T(4,128)} %maximum_bitcast_fusion.own_ref, f32[240,4,256]{2,1,0:T(4,128)} %bitcast.8), custom_call_target="tpu_custom_call" | custom-call | tf_op jit(solution)/shard_map/pallas_call | solution.py:213
  59.2 0.0 copy-start.3
  59.2 10.7 %shard_map.48 = f32[16,256]{1,0:T(8,128)} custom-call(f32[16,256]{1,0:T(8,128)} %get-tuple-element.7.gained_ref, f32[240,256]{1,0:T(8,128)} %get-tuple-element.8.handed_ref), custom_call_target="tpu_custom_call" | custom-call | tf_op jit(solution)/shard_map/pallas_call | solution.py:285
  69.9 0.0 copy-done.3
  69.9 0.8 %select_multiply_fusion = f32[16,256]{1,0:T(8,128)S(1)} fusion(f32[16,256]{1,0:T(8,128)} %shard_map.48, s32[16]{0:T(128)S(1)} %bitcast.13), kind=kLoop, calls=%fused_computation.2 | loop fusion | flops 12288 | bytes 32832 | tf_op jit(solution)/shard_map/mul | solution.py:313
  70.7 0.6 reshape.69
Async XLA Ops:
  0.0 0.7 copy-start.2
  0.7 0.8 %copy-start.1 = (s32[1,1,5,16,2]{3,4,2,1,0:T(2,128)S(1)}, s32[1,1,5,16,2]{3,4,2,1,0:T(2,128)}, u32[]{:S(2)}) copy-start(s32[1,1,5,16,2]{3,4,2,1,0:T(2,128)} %param.7) | copy-start | bytes 1924
  1.5 0.8 %copy-start = (f32[3,1,1,4096]{3,2,1,0:T(1,128)S(1)}, f32[3,1,1,4096]{3,2,1,0:T(1,128)}, u32[]{:S(2)}) copy-start(f32[3,1,1,4096]{3,2,1,0:T(1,128)} %param.4) | copy-start | bytes 147460
  59.2 10.7 %copy-start.3 = (s32[1,1,16]{2,1,0:T(1,128)S(1)}, s32[1,1,16]{2,1,0:T(1,128)}, u32[]{:S(2)}) copy-start(s32[1,1,16]{2,1,0:T(1,128)} %param.6) | copy-start | bytes 196
